TPU v7x, 32 devices: a whole 2x2x4 slice. The times are simulated.
32 devices in a mesh: row: 8 (over z, core), col: 4 (over y, x).
Axes of the slice: x: 2, y: 2, z: 4, core: 2. Of those that a mesh axis runs over, the one named last changes fastest.
Arguments:
- matrix: bfloat16 [4096, 4096], P('row', 'col'), may hold values from -6 to 6
- factors: float32 [4096, 4096], P('row', 'col')
- inverse: bfloat16 [32, 128, 128], P('col'), may hold values from -0.007171631 to 0.007171631
- pattern: int32 [32, 32], P('row', 'col'), may hold values from 0 to 1, as said below
- dropped: int32 [32, 32], P('row', 'col'), may hold values from 0 to 1, as said below
Outputs:
- factors_out: float32 [4096, 4096], P('row', 'col')
Inputs may be any that keep to these rules, and one draw needn't show every extreme that they name: Block (I, J) can be in the pattern only where I - J is 0, 1, -1, 4, -4, 16 or -16; the blocks with I - J of 0, 1, -1, 4 and -4 are always in it. In each device's region of 4 block rows by 8 block columns, every block column holds at most 3 pattern blocks (exactly 3 in some columns), and every block row at most 2 pattern blocks below the block diagonal (exactly 2 in some rows). `dropped`: dropped blocks lie in the pattern and off the block diagonal.
All inputs are finite; a program needn't handle non-finite values.
Results may differ from a plain program's by a relative error of at most 0.00083.
Values may be sent and summed in bfloat16 or wider, within the bound.
A program may use at most 128 MiB of HBM per device.

v0:
```python
import jax
import jax.numpy as jnp
from jax import lax
from jax.sharding import PartitionSpec as P

SWEEPS = 2


def from_behind(block, axis, distance):
    devices = range(lax.axis_size(axis))
    route = [(i - distance, i) for i in devices if i - distance in devices]
    return lax.ppermute(block, axis, route)


def expand(block_mask, block_size):
    return jnp.repeat(jnp.repeat(block_mask, block_size, axis=0), block_size, axis=1)


def on_device(matrix, factors, inverse, pattern, dropped):
    rows_here, cols_here = pattern.shape
    block_size = inverse.shape[1]
    row_devices = lax.axis_size("row")
    row_number = lax.axis_index("row") * rows_here + jnp.arange(rows_here)
    col_number = lax.axis_index("col") * cols_here + jnp.arange(cols_here)
    member = pattern == 1
    below_member = member & (row_number[:, None] > col_number[None, :])
    lower_mask = expand(below_member.astype(jnp.float32), block_size)
    upper_mask = expand(
        (member & (row_number[:, None] <= col_number[None, :])).astype(jnp.float32), block_size
    )
    in_pattern = expand(member.astype(jnp.float32), block_size)
    low_part = factors * lower_mask
    up_part = factors * upper_mask
    dense_matrix = matrix.astype(jnp.float32)
    height = rows_here * block_size
    for sweep_index in range(SWEEPS):
        low_half = low_part.astype(jnp.bfloat16)
        up_half = up_part.astype(jnp.bfloat16)
        lower_panel = lax.all_gather(low_half, "col", axis=1, tiled=True)
        half_axis = row_devices // 2
        before_rows = from_behind(up_half, "row", 1)
        far_rows = from_behind(up_half, "row", half_axis)
        own_start = lax.axis_index("row") * height
        before_start = jnp.maximum(own_start - height, 0)
        far_start = jnp.maximum(own_start - half_axis * height, 0)

        def slice_times(start, shard_rows):
            left_cols = lax.dynamic_slice_in_dim(lower_panel, start, height, 1)
            return jnp.dot(left_cols, shard_rows, preferred_element_type=jnp.float32)

        product = slice_times(own_start, up_half) + slice_times(before_start, before_rows)
        product = product + slice_times(far_start, far_rows)
        residual = (dense_matrix - product - up_part) * in_pattern
        rounded = residual.astype(jnp.bfloat16).reshape(height, cols_here, block_size)
        correction = jnp.einsum(
            "rjb,jbc->rjc", rounded, inverse, preferred_element_type=jnp.float32
        )
        low_part = low_part + correction.reshape(height, cols_here * block_size) * lower_mask
        up_part = up_part + residual * upper_mask
    keep_mask = expand((1 - dropped).astype(jnp.float32), block_size)
    return (low_part + up_part) * keep_mask


def solution(mesh):
    placed = (
        P("row", "col"),
        P("row", "col"),
        P("col", None, None),
        P("row", "col"),
        P("row", "col"),
    )
    return jax.shard_map(
        on_device, mesh=mesh, in_specs=placed, out_specs=P("row", "col"), check_vma=False
    )
```

profile of v0, /device:TPU:20, one launch (start us, length us, event | category | flops | bytes accessed | tf_op | source)
XLA Modules:
  0.0 170.1 jit_solution(9505130866379307461)
XLA Ops:
  6.5 0.7 fusion.36
  7.3 0.1 and_convert_fusion.1
  7.4 0.6 broadcast_in_dim.31
  8.0 0.6 broadcast_in_dim.29
  8.6 0.3 copy-done.3
  9.0 1.8 %fusion.9 = (bf16[512,1024]{1,0:T(8,128)(2,1)}, bf16[512,1024]{1,0:T(8,128)(2,1)S(1)}) fusion(f32[512,1024]{1,0:T(8,128)S(1)} %copy-done.3, f32[64,8,8,128]{3,2,1,0:T(8,128)S(1)} %bitcast.82, f32[64,8,8,128]{3,2,1,0:T(8,128)S(1)} %bitcast.78), kind=kLoop, calls=%fused_computation.18 | loop fusion | flops 2097152 | bytes 8388608 | tf_op jit(solution)/shard_map/convert_element_type | solution.py:37
  10.8 0.0 all-gather.3.cloned.1.call-update
  10.8 0.0 all-gather.5.cloned.1.call-start
  10.9 1.9 %collective-permute-start = (bf16[512,1024]{1,0:T(8,128)(2,1)S(1)}, bf16[512,1024]{1,0:T(8,128)(2,1)}, u32[]{:S(2)}, u32[]{:S(2)}) collective-permute-start(bf16[512,1024]{1,0:T(8,128)(2,1)S(1)} %get-tuple-element.11), channel_id=1, source_target_pairs={{0,4},{4,8},{8,12},{12,16},{16,20},{20,24},{24,28},{1,5},{5,9},{9,... | collective-permute-start | bytes 3145736 | tf_op jit(solution)/shard_map/ppermute | solution.py:12
  12.8 1.3 collective-permute-start.1
  14.1 50.4 %all-gather.3.cloned.1.call-done = bf16[512,4096]{1,0:T(8,128)(2,1)} async-done(((bf16[512,1024]{1,0:T(8,128)(2,1)}), bf16[512,4096]{1,0:T(8,128)(2,1)}) %all-gather.3.cloned.1.call-update) | async-done | bytes 4194320 | tf_op jit(solution)/shard_map/all_gather | solution.py:39
  64.6 1.8 %fusion.25 = f32[512,1024]{1,0:T(8,128)S(1)} fusion(bf16[512,1024]{1,0:T(8,128)(2,1)S(1)} %get-tuple-element.11, bf16[512,4096]{1,0:T(8,128)(2,1)} %all-gather.3.cloned.1.call-done, s32[]{:T(128)S(6)} %select_n.2), kind=kOutput, calls=%fused_computation.36 | convolution fusion | flops 536870912 | bytes 3670020 | tf_op jit(solution)/shard_map/dot_general | solution.py:49
  66.3 0.0 copy-start.10
  66.3 2.3 %fusion.23 = f32[512,1024]{1,0:T(8,128)S(1)} fusion(bf16[512,1024]{1,0:T(8,128)(2,1)} %collective-permute-done, bf16[512,4096]{1,0:T(8,128)(2,1)} %all-gather.3.cloned.1.call-done, s32[]{:T(128)S(6)} %max.8), kind=kOutput, calls=%fused_computation.34 | convolution fusion | flops 536870912 | bytes 3670020 | tf_op jit(solution)/shard_map/dot_general | solution.py:49
  68.7 0.6 broadcast_in_dim.33
  69.3 0.9 copy-done.4
  70.2 2.9 %fusion.1 = f32[512,1024]{1,0:T(8,128)S(1)} fusion(bf16[512,1024]{1,0:T(8,128)(2,1)S(1)} %copy-done.10, f32[512,1024]{1,0:T(8,128)S(1)} %fusion.25, f32[512,1024]{1,0:T(8,128)S(1)} %fusion.23, f32[64,8,8,128]{3,2,1,0:T(8,128)S(1)} %bitcast.85, bf16[512,1024]{1,0:T(8,128)(2,1)} %collective-permute-done.1, f32[512,1024]{1,0:T(8,128)S(1)} %copy-done.4, ...), kind=kOutput, calls=%fused_computation.3 | convolution fusion | flops 540540928 | bytes 15204356 | tf_op jit(solution)/shard_map/dot_general | solution.py:49
  73.2 2.0 %fusion.13 = f32[8,512,128]{1,2,0:T(8,128)} fusion(bf16[8,128,128]{2,1,0:T(8,128)(2,1)S(1)} %copy-done, f32[512,1024]{1,0:T(8,128)S(1)} %fusion.1), kind=kOutput, calls=%fused_computation.22 | convolution fusion | flops 134742016 | bytes 4456448 | tf_op jit(solution)/shard_map/rjb,jbc->rjc/dot_general | solution.py:55
  75.2 3.0 %copy.14 = f32[512,1024]{1,0:T(8,128)} copy(f32[512,1024]{0,1:T(8,128)} %bitcast.88) | data formatting | bytes 4194304 | tf_op jit(solution)/shard_map/reshape | solution.py:58
  78.2 6.9 %fusion.34 = (bf16[512,1024]{1,0:T(8,128)(2,1)S(1)}, f32[512,1024]{1,0:T(8,128)}, bf16[512,1024]{1,0:T(8,128)(2,1)}) fusion(f32[512,1024]{1,0:T(8,128)} %copy-done.9, f32[512,1024]{1,0:T(8,128)} %param.6, f32[64,8,8,128]{3,2,1,0:T(8,128)S(1)} %bitcast.80, f32[512,1024]{1,0:T(8,128)} %copy.14, f32[64,8,8,128]{3,2,1,0:T(8,128)} %bitcast.83), kind=kLoop, calls=%fused_computation.51 | loop fusion | flops 4194304 | bytes 14680064 | tf_op jit(solution)/shard_map/convert_element_type | solution.py:38
  85.1 0.0 all-gather.5.cloned.1.call-update
  85.1 1.9 %collective-permute-start.2 = (bf16[512,1024]{1,0:T(8,128)(2,1)S(1)}, bf16[512,1024]{1,0:T(8,128)(2,1)}, u32[]{:S(2)}, u32[]{:S(2)}) collective-permute-start(bf16[512,1024]{1,0:T(8,128)(2,1)S(1)} %get-tuple-element.5), channel_id=1, source_target_pairs={{0,4},{4,8},{8,12},{12,16},{16,20},{20,24},{24,28},{1,5},{5,9},{9,... | collective-permute-start | bytes 3145736 | tf_op jit(solution)/shard_map/ppermute | solution.py:12
  87.1 1.5 collective-permute-start.3
  88.6 52.9 %all-gather.5.cloned.1.call-done = bf16[512,4096]{1,0:T(8,128)(2,1)} async-done(((bf16[512,1024]{1,0:T(8,128)(2,1)}), bf16[512,4096]{1,0:T(8,128)(2,1)}) %all-gather.5.cloned.1.call-update) | async-done | bytes 4194320 | tf_op jit(solution)/shard_map/all_gather | solution.py:39
  141.4 1.9 %fusion.20 = f32[512,1024]{1,0:T(8,128)S(1)} fusion(bf16[512,1024]{1,0:T(8,128)(2,1)S(1)} %get-tuple-element.5, bf16[512,4096]{1,0:T(8,128)(2,1)} %all-gather.5.cloned.1.call-done, s32[]{:T(128)S(6)} %select_n.2), kind=kOutput, calls=%fused_computation.31 | convolution fusion | flops 536870912 | bytes 3670020 | tf_op jit(solution)/shard_map/dot_general | solution.py:49
  143.4 2.3 %fusion.18 = f32[512,1024]{1,0:T(8,128)S(1)} fusion(bf16[512,1024]{1,0:T(8,128)(2,1)} %collective-permute-done.2, bf16[512,4096]{1,0:T(8,128)(2,1)} %all-gather.5.cloned.1.call-done, s32[]{:T(128)S(6)} %max.8), kind=kOutput, calls=%fused_computation.29 | convolution fusion | flops 536870912 | bytes 3670020 | tf_op jit(solution)/shard_map/dot_general | solution.py:49
  145.8 2.7 %fusion.3 = f32[512,1024]{1,0:T(8,128)S(1)} fusion(f32[512,1024]{1,0:T(8,128)S(1)} %copy-done.5, bf16[512,1024]{1,0:T(8,128)(2,1)S(1)} %copy-done.11, f32[512,1024]{1,0:T(8,128)S(1)} %fusion.20, f32[512,1024]{1,0:T(8,128)S(1)} %fusion.18, f32[64,8,8,128]{3,2,1,0:T(8,128)S(1)} %bitcast.86, bf16[512,1024]{1,0:T(8,128)(2,1)} %collective-permute-done.3, ...), kind=kOutput, calls=%fused_computation.5 | convolution fusion | flops 540016640 | bytes 13107204 | tf_op jit(solution)/shard_map/dot_general | solution.py:49
  148.5 2.0 %fusion.10 = f32[8,512,128]{1,2,0:T(8,128)} fusion(bf16[8,128,128]{2,1,0:T(8,128)(2,1)S(1)} %copy-done, f32[512,1024]{1,0:T(8,128)S(1)} %fusion.3), kind=kOutput, calls=%fused_computation.19 | convolution fusion | flops 134742016 | bytes 4456448 | tf_op jit(solution)/shard_map/rjb,jbc->rjc/dot_general | solution.py:55
  150.6 2.9 %copy.15 = f32[512,1024]{1,0:T(8,128)} copy(f32[512,1024]{0,1:T(8,128)} %bitcast.89) | data formatting | bytes 4194304 | tf_op jit(solution)/shard_map/reshape | solution.py:58
  153.5 0.6 broadcast_in_dim.35
  154.1 1.0 copy-done.2
  155.0 8.2 %bitcast_multiply_fusion = f32[512,1024]{1,0:T(8,128)} fusion(f32[64,8,8,128]{3,2,1,0:T(8,128)S(1)} %bitcast.87, f32[512,1024]{1,0:T(8,128)} %get-tuple-element.6, f32[512,1024]{1,0:T(8,128)} %copy-done.6, f32[512,1024]{1,0:T(8,128)} %copy.15, f32[64,8,8,128]{3,2,1,0:T(8,128)S(1)} %bitcast.81, f32[64,8,8,128]{3,2,1,0:T(8,128)S(1)} %bitcast.84, ...), kind=kLoop, calls=%fused_computation.6 | loop fusion | flops 4718592 | bytes 18874368 | tf_op jit(solution)/shard_map/mul | solution.py:61
  (34 shorter events, 0.2 us)
Async XLA Ops:
  6.5 66.6 %copy-start = (bf16[8,128,128]{2,1,0:T(8,128)(2,1)S(1)}, bf16[8,128,128]{2,1,0:T(8,128)(2,1)}, u32[]{:S(2)}) copy-start(bf16[8,128,128]{2,1,0:T(8,128)(2,1)} %param.7) | copy-start | bytes 786436
  6.5 58.0 %all-gather.3.cloned.1.call-start = ((), (), s32[]{:S(2)}) async-start(), calls=%async_computation | async-start | bytes 5242880 | tf_op jit(solution)/shard_map/all_gather | solution.py:39
  7.4 1.6 copy-start.3
  8.6 2.2 %copy-start.1 = (f32[512,8,128]{2,1,0:T(8,128)}, f32[512,8,128]{2,1,0:T(8,128)S(1)}, u32[]{:S(2)}) copy-start(f32[512,8,128]{2,1,0:T(8,128)S(1)} %broadcast_in_dim.29) | copy-start | bytes 6291460
  10.8 130.6 %all-gather.5.cloned.1.call-start = ((), (), s32[]{:S(2)}) async-start(), calls=%async_computation.1 | async-start | bytes 5242880 | tf_op jit(solution)/shard_map/all_gather | solution.py:39
  10.9 55.4 %collective-permute-start = (bf16[512,1024]{1,0:T(8,128)(2,1)S(1)}, bf16[512,1024]{1,0:T(8,128)(2,1)}, u32[]{:S(2)}, u32[]{:S(2)}) collective-permute-start(bf16[512,1024]{1,0:T(8,128)(2,1)S(1)} %get-tuple-element.11), channel_id=1, source_target_pairs={{0,4},{4,8},{8,12},{12,16},{16,20},{20,24},{24,28},{1,5},{5,9},{9,... | collective-permute-start | bytes 3145736 | tf_op jit(solution)/shard_map/ppermute | solution.py:12
  12.8 55.8 %collective-permute-start.1 = (bf16[512,1024]{1,0:T(8,128)(2,1)S(1)}, bf16[512,1024]{1,0:T(8,128)(2,1)}, u32[]{:S(2)}, u32[]{:S(2)}) collective-permute-start(bf16[512,1024]{1,0:T(8,128)(2,1)S(1)} %get-tuple-element.11), channel_id=1, source_target_pairs={{0,16},{4,20},{8,24},{12,28},{1,17},{5,21},{9,25},{13,29},{2,18},{... | collective-permute-start | bytes 3145736 | tf_op jit(solution)/shard_map/ppermute | solution.py:12
  66.3 3.0 %copy-start.10 = (bf16[512,1024]{1,0:T(8,128)(2,1)S(1)}, bf16[512,1024]{1,0:T(8,128)(2,1)}, u32[]{:S(2)}) copy-start(bf16[512,1024]{1,0:T(8,128)(2,1)} %param.5) | copy-start | bytes 3145732
  68.6 1.6 copy-start.4
  69.3 3.9 %copy-start.7 = (f32[512,8,128]{2,1,0:T(8,128)}, f32[512,8,128]{2,1,0:T(8,128)S(1)}, u32[]{:S(2)}) copy-start(f32[512,8,128]{2,1,0:T(8,128)S(1)} %broadcast_in_dim.33) | copy-start | bytes 6291460
  73.2 2.0 %copy-start.9 = (f32[512,1024]{1,0:T(8,128)}, f32[512,1024]{1,0:T(8,128)S(1)}, u32[]{:S(2)}) copy-start(f32[512,1024]{1,0:T(8,128)S(1)} %fusion.1) | copy-start | bytes 6291460
  78.2 10.4 %copy-start.12 = (s32[4,8]{1,0:T(4,128)S(1)}, s32[4,8]{1,0:T(4,128)}, u32[]{:S(2)}) copy-start(s32[4,8]{1,0:T(4,128)} %param.9) | copy-start | bytes 388
  85.1 58.2 %collective-permute-start.2 = (bf16[512,1024]{1,0:T(8,128)(2,1)S(1)}, bf16[512,1024]{1,0:T(8,128)(2,1)}, u32[]{:S(2)}, u32[]{:S(2)}) collective-permute-start(bf16[512,1024]{1,0:T(8,128)(2,1)S(1)} %get-tuple-element.5), channel_id=1, source_target_pairs={{0,4},{4,8},{8,12},{12,16},{16,20},{20,24},{24,28},{1,5},{5,9},{9,... | collective-permute-start | bytes 3145736 | tf_op jit(solution)/shard_map/ppermute | solution.py:12
  87.1 58.7 %collective-permute-start.3 = (bf16[512,1024]{1,0:T(8,128)(2,1)S(1)}, bf16[512,1024]{1,0:T(8,128)(2,1)}, u32[]{:S(2)}, u32[]{:S(2)}) collective-permute-start(bf16[512,1024]{1,0:T(8,128)(2,1)S(1)} %get-tuple-element.5), channel_id=1, source_target_pairs={{0,16},{4,20},{8,24},{12,28},{1,17},{5,21},{9,25},{13,29},{2,18},{... | collective-permute-start | bytes 3145736 | tf_op jit(solution)/shard_map/ppermute | solution.py:12
  141.4 4.3 %copy-start.8 = (f32[512,8,128]{2,1,0:T(8,128)S(1)}, f32[512,8,128]{2,1,0:T(8,128)}, u32[]{:S(2)}) copy-start(f32[512,8,128]{2,1,0:T(8,128)} %copy-done.7) | copy-start | bytes 6291460
  143.3 2.4 %copy-start.5 = (f32[512,1024]{1,0:T(8,128)S(1)}, f32[512,1024]{1,0:T(8,128)}, u32[]{:S(2)}) copy-start(f32[512,1024]{1,0:T(8,128)} %get-tuple-element.6) | copy-start | bytes 6291460
  143.3 2.4 %copy-start.11 = (bf16[512,1024]{1,0:T(8,128)(2,1)S(1)}, bf16[512,1024]{1,0:T(8,128)(2,1)}, u32[]{:S(2)}) copy-start(bf16[512,1024]{1,0:T(8,128)(2,1)} %param.5) | copy-start | bytes 3145732
  148.5 2.1 %copy-start.6 = (f32[512,1024]{1,0:T(8,128)}, f32[512,1024]{1,0:T(8,128)S(1)}, u32[]{:S(2)}) copy-start(f32[512,1024]{1,0:T(8,128)S(1)} %fusion.3) | copy-start | bytes 6291460
  153.4 1.6 copy-start.2
Sparse Core Ops, SparseCore 0:
  10.9 53.5 all-gather.2
  85.2 56.1 all-gather.4
where the time goes:
time: 172 us; the launch traced here: 170 us
  waiting for transfers between devices  103 us (60%)
  matrix products  18 us (10%)
  other arithmetic  17.8 us (10%)
  between operations  13.7 us (8%)
  local copies, waits for them, and re-layouts  10.6 us (6%)
  starting transfers between devices  6.65 us (4%)
    all_gather x2, waiting for transfers between devices, on_device(): lower_panel = lax.all_gather(low_half, 'col', axis=1, tiled=True)  103 us
    dot_general x6, matrix products, slice_times(): return jnp.dot(left_cols, shard_rows, preferred_element_type=jnp.float32)  14 us
    mul x1, other arithmetic, on_device(): return (low_part + up_part) * keep_mask  8.25 us
    convert_element_type x1, other arithmetic, on_device(): up_half = up_part.astype(jnp.bfloat16)  6.91 us
    ppermute x4, starting transfers between devices, from_behind(): return lax.ppermute(block, axis, route)  6.61 us
    reshape x2, local copies, waits for them, and re-layouts, on_device(): correction.reshape(height, cols_here * block_size) * lower_mask  5.86 us
    dot_general x2, matrix products, on_device(): jnp.einsum('rjb,jbc->rjc', rounded, inverse, preferred_element_type=jnp.f...  4.06 us
  transfers between devices with their start and end apart: 6, of which 2 were waited for; matrix products, arithmetic and copies ran while one was open for 5% of the time, Pallas kernels for 0%

commit v1 on v0

v1 whole, which is shorter than its diff:
```python
import functools

import jax
import jax.numpy as jnp
from jax import lax
from jax.experimental import pallas as pl
from jax.experimental.pallas import tpu as pltpu
from jax.sharding import PartitionSpec as P

SWEEPS = 2
MESH = pl.DeviceIdType.MESH
F32 = jnp.float32
BF16 = jnp.bfloat16

SLOTS = 4
DIAG, LEFT, RIGHT, OUTER = range(SLOTS)
D_NEAR, D_FAR, L_NEAR, U_NEAR, L_FAR, U_FAR = range(6)


def dot(x, y):
    return jnp.dot(x, y, preferred_element_type=F32)


def sweep_kernel(
    rows, cols, row_devices, col_devices, bs,
    pattern, dropped, matrix, factors, inverse_in, out,
    a, inverse, lb, ub, sd, rd, rln, run, rlf, ruf, acc,
    load_sem, inverse_sem, send_sem, recv_sem,
):
    r, c = lax.axis_index("row"), lax.axis_index("col")
    far_r, far_c = row_devices // 2, col_devices // 2
    q = r - (cols // rows) * c
    barrier = pltpu.get_barrier_semaphore()

    def loads(i, s, j):
        k = i * SLOTS + s
        src = (pl.ds(i * bs, bs), pl.ds(pl.multiple_of(j * bs, bs), bs))
        return (
            pltpu.make_async_copy(factors.at[src], out.at[k], load_sem.at[0, k]),
            pltpu.make_async_copy(matrix.at[src], a.at[k], load_sem.at[1, k]),
        )

    def start_loads(blocks):
        for block in blocks:
            for copy in loads(*block):
                copy.start()

    def wait_loads(blocks):
        for block in blocks:
            for copy in loads(*block):
                copy.wait()

    inverse_copy = pltpu.make_async_copy(inverse_in, inverse, inverse_sem)

    def hello(r2, c2):
        pl.semaphore_signal(barrier, inc=1, device_id=(r2, c2), device_id_type=MESH)

    def message(kind, v, src, dst, slot, r2, c2):
        return pltpu.make_async_remote_copy(
            src_ref=src, dst_ref=dst,
            send_sem=send_sem.at[kind, v], recv_sem=recv_sem.at[slot, v],
            device_id=(r2, c2), device_id_type=MESH,
        )

    def d_near(v):
        return message(D_NEAR, v, sd.at[v], rd.at[v], D_NEAR, r + 1, c)

    def d_far(v):
        return message(D_FAR, v, sd.at[v], rd.at[v], D_NEAR, r + far_r, c)

    def l_near(v):
        return message(L_NEAR, v, lb.at[v, pl.ds(0, rows + 1)], rln.at[v], L_NEAR, r, c + 1)

    def u_near(v):
        return message(U_NEAR, v, ub.at[v, pl.ds(0, rows + 1)], run.at[v], U_NEAR, r + 1, c)

    def l_far(v):
        return message(L_FAR, v, lb.at[v, pl.ds(0, rows)], rlf.at[v], L_FAR, r, c + far_c)

    def u_far(v):
        return message(U_FAR, v, ub.at[v, pl.ds(0, rows)], ruf.at[v], U_FAR, r + far_r, c)

    def lower_step(k, b, v, diag, j, mask=None):
        product = dot(lb[v, b], diag)
        residual = a[k].astype(F32) - product
        if mask is not None:
            residual = residual * mask
        correction = dot(residual.astype(BF16), inverse[j])
        if mask is not None:
            correction = correction * mask
        out[k] = out[k] + correction
        if v + 1 < SWEEPS:
            lb[v + 1, b] = out[k].astype(BF16)

    def upper_steps(k, b, mask=None):
        for v in range(SWEEPS):
            ub[v, b] = out[k].astype(BF16)
            residual = a[k].astype(F32) - out[k]
            if mask is not None:
                residual = residual * mask
            out[k] = out[k] + residual

    def keep(i, s, j):
        k = i * SLOTS + s
        out[k] = out[k] * (1 - dropped[i, j]).astype(F32)

    out[rows * SLOTS] = jnp.zeros((bs, bs), F32)

    def diagonal_owner(h):
        base = h * rows
        below = [(i, LEFT, base + i - 1) for i in range(rows) if base + i >= 1]
        right = [(i, RIGHT, base + i + 1) for i in range(rows) if base + i + 1 < cols]
        diag = [(i, DIAG, base + i) for i in range(rows)]
        outer = [(i, OUTER, i if h else rows + i) for i in range(rows)]
        has_far = c >= far_c
        sends_far = c < far_c
        has_near = c >= 1
        sends_near = c + 1 < col_devices

        def when_near_in(f):
            if h:
                f()
            else:
                pl.when(has_near)(f)

        def when_near_out(f):
            if h:
                pl.when(sends_near)(f)
            else:
                f()

        start_loads(diag)
        start_loads(outer)
        start_loads(right)
        start_loads(below)
        inverse_copy.start()

        def hello_near():
            hello(r - 1, c)
            if not h:
                hello(r, c - 1)

        when_near_in(hello_near)

        @pl.when(has_far)
        def _():
            hello(r - far_r, c)
            hello(r, c - far_c)

        wait_loads(diag)
        for i in range(rows):
            sd[0, i] = out[i * SLOTS + DIAG].astype(BF16)
        near_peers = sends_near.astype(jnp.int32) if h else 1
        peers = near_peers + sends_far.astype(jnp.int32)
        pl.when(peers > 0)(lambda: pl.semaphore_wait(barrier, peers))

        def send_d(v):
            pl.when(sends_far)(lambda: d_far(v).start())
            when_near_out(lambda: d_near(v).start())

        send_d(0)
        wait_loads(outer)
        wait_loads(right)
        for i, s, j in right:
            upper_steps(i * SLOTS + s, 2 * rows - 1 - i)
        if not h:
            for i, s, j in outer:
                upper_steps(i * SLOTS + s, i)
            u_near(0).start()
            u_near(1).start()
        wait_loads(below)
        for i, s, j in below:
            lb[0, rows + i] = out[i * SLOTS + s].astype(BF16)
        if h:
            for i, s, j in outer:
                lb[0, i] = out[i * SLOTS + s].astype(BF16)
        inverse_copy.wait()

        for v in range(SWEEPS):
            acc[0] = jnp.zeros((bs, bs), F32)
            for i in range(1, rows):
                acc[i] = dot(lb[v, rows + i], ub[v, 2 * rows - i])

            def near_terms():
                u_near_in = message(U_NEAR, v, ub.at[v, pl.ds(0, rows + 1)], run.at[v], U_NEAR, r - 1, c)
                u_near_in.wait_recv()
                if h:
                    left = lb
                else:
                    message(L_NEAR, v, lb.at[v, pl.ds(0, rows + 1)], rln.at[v], L_NEAR, r, c - 1).wait_recv()
                    left = rln
                acc[0] = acc[0] + dot(left[v, rows], run[v, rows])
                for i in range(rows):
                    acc[i] = acc[i] + dot(left[v, i], run[v, i])

            def far_terms():
                message(U_FAR, v, ub.at[v, pl.ds(0, rows)], ruf.at[v], U_FAR, r - far_r, c).wait_recv()
                message(L_FAR, v, lb.at[v, pl.ds(0, rows)], rlf.at[v], L_FAR, r, c - far_c).wait_recv()
                for i in range(rows):
                    acc[i] = acc[i] + dot(rlf[v, i], ruf[v, i])

            def local_lower():
                for i in range(1, rows):
                    lower_step(i * SLOTS + LEFT, rows + i, v, sd[v, i - 1], base + i - 1)

            def lower_from_before():
                if h:
                    message(D_NEAR, v, sd.at[v], rd.at[v], D_NEAR, r - 1, c).wait_recv()
                    lower_step(LEFT, rows, v, rd[v, rows - 1], rows - 1)
                    for i in range(rows):
                        lower_step(i * SLOTS + OUTER, i, v, rd[v, i], i)

            def diag_step():
                for i in range(rows):
                    k = i * SLOTS + DIAG
                    residual = a[k].astype(F32) - acc[i] - out[k]
                    out[k] = out[k] + residual
                    if v + 1 < SWEEPS:
                        sd[v + 1, i] = out[k].astype(BF16)
                if v + 1 < SWEEPS:
                    send_d(v + 1)

            local_lower()
            when_near_in(near_terms)
            if v + 1 < SWEEPS:
                pl.when(has_far)(far_terms)
                diag_step()
                lower_from_before()
            else:
                lower_from_before()
                pl.when(has_far)(far_terms)
                diag_step()

        for i, s, j in below + right + outer:
            keep(i, s, j)
        for v in range(SWEEPS):
            when_near_out(lambda: d_near(v).wait_send())
            pl.when(sends_far)(lambda: d_far(v).wait_send())
            if not h:
                u_near(v).wait_send()

    def lower_owner(blocks, source_r, l_message, far):
        places = [(i, s, j) for i, s, j, b, n in blocks]
        start_loads(places)
        inverse_copy.start()
        hello(source_r, c)
        wait_loads(places)
        masks = {}
        for i, s, j, b, n in blocks:
            k = i * SLOTS + s
            masks[k] = pattern[i, j].astype(F32) if far else None
            if far:
                out[k] = out[k] * masks[k]
            lb[0, b] = out[k].astype(BF16)
        pl.semaphore_wait(barrier, 1)
        l_message(0).start()
        inverse_copy.wait()
        for v in range(SWEEPS):
            message(D_NEAR, v, sd.at[v], rd.at[v], D_NEAR, source_r, c).wait_recv()
            for i, s, j, b, n in blocks:
                k = i * SLOTS + s
                lower_step(k, b, v, rd[v, n], j, masks[k])
            if v + 1 < SWEEPS:
                l_message(v + 1).start()
        for i, s, j in places:
            keep(i, s, j)
        for v in range(SWEEPS):
            l_message(v).wait_send()

    def upper_owner(blocks, u_message, far):
        places = [(i, s, j) for i, s, j, b in blocks]
        start_loads(places)
        wait_loads(places)
        for i, s, j, b in blocks:
            k = i * SLOTS + s
            mask = pattern[i, j].astype(F32) if far else None
            if far:
                out[k] = out[k] * mask
            upper_steps(k, b, mask)
        pl.semaphore_wait(barrier, 1)
        for v in range(SWEEPS):
            u_message(v).start()
        for i, s, j in places:
            keep(i, s, j)
        for v in range(SWEEPS):
            u_message(v).wait_send()

    pl.when(q == 0)(lambda: diagonal_owner(0))
    pl.when(q == 1)(lambda: diagonal_owner(1))

    @pl.when(q == 2)
    def _():
        blocks = [(i, OUTER, rows + i, i, i) for i in range(rows)]
        lower_owner(blocks + [(0, LEFT, cols - 1, rows, rows - 1)], r - 1, l_near, False)

    @pl.when(q == -1)
    def _():
        blocks = [(i, OUTER, i, i) for i in range(rows)]
        upper_owner(blocks + [(rows - 1, RIGHT, 0, rows)], u_near, False)

    @pl.when((q == far_r) | (q == far_r + 1))
    def _():
        base = (q - far_r) * rows
        blocks = [(i, OUTER, base + i, i, i) for i in range(rows)]
        lower_owner(blocks, r - far_r, l_far, True)

    @pl.when((q == -far_r) | (q == 1 - far_r))
    def _():
        base = (q + far_r) * rows
        blocks = [(i, OUTER, base + i, i) for i in range(rows)]
        upper_owner(blocks, u_far, True)


def place_kernel(rows, cols, row_devices, bs, blocks, out, sem):
    r, c = lax.axis_index("row"), lax.axis_index("col")
    q = r - (cols // rows) * c
    far = (row_devices // 2) * rows
    copies = []
    for i in range(rows):
        for j in range(cols):
            d = rows * q + i - j
            k = jnp.where(
                d == 0, i * SLOTS + DIAG,
                jnp.where(
                    d == 1, i * SLOTS + LEFT,
                    jnp.where(
                        d == -1, i * SLOTS + RIGHT,
                        jnp.where(
                            (d == rows) | (d == -rows) | (d == far) | (d == -far),
                            i * SLOTS + OUTER, rows * SLOTS,
                        ),
                    ),
                ),
            )
            dst = out.at[pl.ds(i * bs, bs), pl.ds(j * bs, bs)]
            copies.append(pltpu.make_async_copy(blocks.at[k], dst, sem.at[i * cols + j]))
    for copy in copies:
        copy.start()
    for copy in copies:
        copy.wait()


def solution(mesh):
    row_devices, col_devices = mesh.shape["row"], mesh.shape["col"]

    def on_device(matrix, factors, inverse, pattern, dropped):
        rows, cols = pattern.shape
        bs = inverse.shape[1]
        places = rows * SLOTS
        half = lambda *n: pltpu.VMEM(n + (bs, bs), BF16)
        hbm = pl.BlockSpec(memory_space=pl.ANY)
        smem = pl.BlockSpec(memory_space=pltpu.SMEM)
        vmem = pl.BlockSpec(memory_space=pltpu.VMEM)
        blocks = pl.pallas_call(
            functools.partial(sweep_kernel, rows, cols, row_devices, col_devices, bs),
            out_shape=jax.ShapeDtypeStruct((places + 1, bs, bs), F32),
            in_specs=[smem, smem, hbm, hbm, hbm],
            out_specs=vmem,
            scratch_shapes=[
                half(places), half(cols), half(SWEEPS, 2 * rows), half(SWEEPS, 2 * rows),
                half(SWEEPS, rows), half(SWEEPS, rows),
                half(SWEEPS, rows + 1), half(SWEEPS, rows + 1), half(SWEEPS, rows), half(SWEEPS, rows),
                pltpu.VMEM((rows, bs, bs), F32),
                pltpu.SemaphoreType.DMA((2, places)),
                pltpu.SemaphoreType.DMA,
                pltpu.SemaphoreType.DMA((6, SWEEPS)),
                pltpu.SemaphoreType.DMA((6, SWEEPS)),
            ],
            compiler_params=pltpu.CompilerParams(collective_id=0, has_side_effects=True),
            name="sweeps",
        )(pattern, dropped, matrix, factors, inverse)
        return pl.pallas_call(
            functools.partial(place_kernel, rows, cols, row_devices, bs),
            out_shape=jax.ShapeDtypeStruct(factors.shape, F32),
            in_specs=[vmem],
            out_specs=hbm,
            scratch_shapes=[pltpu.SemaphoreType.DMA((rows * cols,))],
            name="place",
        )(blocks)

    placed = (P("row", "col"), P("row", "col"), P("col", None, None), P("row", "col"), P("row", "col"))
    return jax.shard_map(
        on_device, mesh=mesh, in_specs=placed, out_specs=P("row", "col"), check_vma=False
    )
```

time: 172 us -> 18.6 us (0.11)
  waiting for transfers between devices: 103 us -> 0 us
  Pallas kernels: 0 us -> 18.4 us
  matrix products: 18 us -> 0 us
  other arithmetic: 17.8 us -> 0 us
  between operations: 13.7 us -> 0.01 us
  local copies, waits for them, and re-layouts: 10.6 us -> 0 us
  starting transfers between devices: 6.65 us -> 0 us
    all_gather x2 -> x0, waiting for transfers between devices: 103 us -> none  [on_device(): lower_panel = lax.all_gather(low_half, 'col', axis=1, tiled=True)]
    pallas_call x0 -> x2, Pallas kernels: none -> 18.4 us  [the longest x1 15.6 us: on_device(): pl.pallas_call(functools.partial(sweep_kernel, rows, cols, row_devices, c...]
    dot_general x8 -> x0, matrix products: 18 us -> none  [the longest x6 14 us: slice_times(): return jnp.dot(left_cols, shard_rows, preferred_element_type=jnp.float32)]
    convert_element_type x5 -> x0, other arithmetic: 9.54 us -> none  [the longest x1 6.91 us: on_device(): up_half = up_part.astype(jnp.bfloat16)]
    mul x1 -> x0, other arithmetic: 8.25 us -> none  [on_device(): return (low_part + up_part) * keep_mask]
    ppermute x4 -> x0, starting transfers between devices: 6.61 us -> none  [from_behind(): return lax.ppermute(block, axis, route)]
    reshape x2 -> x0, local copies, waits for them, and re-layouts: 5.86 us -> none  [on_device(): correction.reshape(height, cols_here * block_size) * lower_mask]
    broadcast_in_dim x8 -> x0, local copies, waits for them, and re-layouts: 2.48 us -> none  [the longest x4 2.4 us: expand(): jnp.repeat(jnp.repeat(block_mask, block_size, axis=0), block_size, axis=1)]
  transfers between devices with their start and end apart: 6 -> 0, of which waited for: 2 -> 0; matrix products, arithmetic and copies ran while one was open for 5% -> 0% of each run, Pallas kernels for 0% -> 0%
where the time goes in v1:
time: 18.6 us; the launch traced here: 18.4 us
  Pallas kernels  18.4 us (99%)
    pallas_call x1, Pallas kernels, on_device(): pl.pallas_call(functools.partial(sweep_kernel, rows, cols, row_devices, c...  15.6 us
    pallas_call x1, Pallas kernels, on_device(): pl.pallas_call(functools.partial(place_kernel, rows, cols, row_devices, b...  2.81 us

profile of v1, /device:TPU:20, one launch (start us, length us, event | category | flops | bytes accessed | tf_op | source)
XLA Modules:
  0.0 18.4 jit_solution(7815382553992503352)
XLA Ops:
  0.0 15.6 %sweeps.1.blocks = f32[17,128,128]{2,1,0:T(8,128)} custom-call(s32[4,8]{1,0:T(4,128)} %pattern.1, s32[4,8]{1,0:T(4,128)} %dropped.1, bf16[512,1024]{1,0:T(8,128)(2,1)} %matrix.1, f32[512,1024]{1,0:T(8,128)} %factors.1, bf16[8,128,128]{2,1,0:T(8,128)(2,1)} %inverse_in.1), custom_call_target="tpu_custom_call" | custom-call | tf_op jit(solution)/shard_map/sweeps/pallas_call | solution.py:354
  15.6 2.8 %place.1 = f32[512,1024]{1,0:T(8,128)} custom-call(f32[17,128,128]{2,1,0:T(8,128)} %sweeps.1.blocks), custom_call_target="tpu_custom_call" | custom-call | tf_op jit(solution)/shard_map/place/pallas_call | solution.py:372

commit v2 on v1

v2 whole, which is shorter than its diff:
```python
import functools

import jax
import jax.numpy as jnp
from jax import lax
from jax.experimental import pallas as pl
from jax.experimental.pallas import tpu as pltpu
from jax.sharding import PartitionSpec as P

SWEEPS = 2
MESH = pl.DeviceIdType.MESH
F32 = jnp.float32
BF16 = jnp.bfloat16

SLOTS = 4
DIAG, LEFT, RIGHT, OUTER = range(SLOTS)
D_NEAR, D_FAR, L_NEAR, U_NEAR, L_FAR, U_FAR = range(6)


def dot(x, y):
    return jnp.dot(x, y, preferred_element_type=F32)


def sweep_kernel(
    rows, cols, row_devices, col_devices, bs,
    pattern, dropped, matrix, factors, inverse_in, out,
    a, inverse, lb, ub, ua, sd, rd, rln, run, rlf, ruf, acc,
    load_sem, inverse_sem, send_sem, recv_sem,
):
    r, c = lax.axis_index("row"), lax.axis_index("col")
    far_r, far_c = row_devices // 2, col_devices // 2
    q = r - (cols // rows) * c
    barrier = pltpu.get_barrier_semaphore()

    def loads(i, s, j):
        k = s * rows + i
        src = (pl.ds(i * bs, bs), pl.ds(pl.multiple_of(j * bs, bs), bs))
        return (
            pltpu.make_async_copy(factors.at[src], out.at[k], load_sem.at[0, k]),
            pltpu.make_async_copy(matrix.at[src], a.at[k], load_sem.at[1, k]),
        )

    def start_loads(blocks):
        for block in blocks:
            for copy in loads(*block):
                copy.start()

    def wait_loads(blocks):
        for block in blocks:
            for copy in loads(*block):
                copy.wait()

    inverse_copy = pltpu.make_async_copy(inverse_in, inverse, inverse_sem)

    def hello(r2, c2):
        pl.semaphore_signal(barrier, inc=1, device_id=(r2, c2), device_id_type=MESH)

    def message(kind, v, b, src, dst, slot, r2, c2):
        return pltpu.make_async_remote_copy(
            src_ref=src, dst_ref=dst.at[v, b],
            send_sem=send_sem.at[kind, v, b], recv_sem=recv_sem.at[slot, v, b],
            device_id=(r2, c2), device_id_type=MESH,
        )

    def receive(slot, v, b, dst, r2, c2):
        message(slot, v, b, dst.at[v, b], dst, slot, r2, c2).wait_recv()

    def d_near(v, b):
        return message(D_NEAR, v, b, sd.at[v, b], rd, D_NEAR, r + 1, c)

    def d_far(v, b):
        return message(D_FAR, v, b, sd.at[v, b], rd, D_NEAR, r + far_r, c)

    def l_near(v, b):
        return message(L_NEAR, v, b, lb.at[v, b], rln, L_NEAR, r, c + 1)

    def l_far(v, b):
        return message(L_FAR, v, b, lb.at[v, b], rlf, L_FAR, r, c + far_c)

    def u_near(v, b):
        k = OUTER * rows + b if b < rows else RIGHT * rows + rows - 1
        src = a.at[k] if v else ub.at[b]
        return message(U_NEAR, v, b, src, run, U_NEAR, r + 1, c)

    def u_far(v, b):
        src = ua.at[b] if v else ub.at[b]
        return message(U_FAR, v, b, src, ruf, U_FAR, r + far_r, c)

    def kept(i, j):
        return (1 - dropped[i, j]).astype(F32)

    def lower_step(i, s, j, b, v, diag, mask=None):
        k = s * rows + i
        residual = a[k].astype(F32) - dot(lb[v, b], diag)
        if mask is not None:
            residual = residual * mask
        correction = dot(residual.astype(BF16), inverse[j])
        if mask is not None:
            correction = correction * mask
        new = out[k] + correction
        if v + 1 < SWEEPS:
            out[k] = new
            lb[v + 1, b] = new.astype(BF16)
        else:
            out[k] = new * kept(i, j)

    out[rows * SLOTS] = jnp.zeros((bs, bs), F32)

    def diagonal_owner(h):
        base = h * rows
        below = [(i, LEFT, base + i - 1) for i in range(rows) if base + i >= 1]
        right = [(i, RIGHT, base + i + 1) for i in range(rows) if base + i + 1 < cols]
        diag = [(i, DIAG, base + i) for i in range(rows)]
        outer = [(i, OUTER, i if h else rows + i) for i in range(rows)]
        has_far = c >= far_c
        sends_far = c < far_c
        has_near = c >= 1
        sends_near = c + 1 < col_devices

        def when_near_in(f):
            if h:
                f()
            else:
                pl.when(has_near)(f)

        def when_near_out(f):
            if h:
                pl.when(sends_near)(f)
            else:
                f()

        start_loads(diag)
        start_loads(outer)
        start_loads(right)
        start_loads(below)
        inverse_copy.start()

        def hello_near():
            hello(r - 1, c)
            if not h:
                hello(r, c - 1)

        when_near_in(hello_near)

        @pl.when(has_far)
        def _():
            hello(r - far_r, c)
            hello(r, c - far_c)

        wait_loads(diag)
        for i in range(rows):
            sd[0, i] = out[DIAG * rows + i].astype(BF16)
        near_peers = sends_near.astype(jnp.int32) if h else 1
        peers = near_peers + sends_far.astype(jnp.int32)
        pl.when(peers > 0)(lambda: pl.semaphore_wait(barrier, peers))

        @pl.when(sends_far)
        def _():
            for b in range(rows):
                d_far(0, b).start()

        def send_first_near():
            for b in range(rows):
                d_near(0, b).start()

        when_near_out(send_first_near)
        wait_loads(outer)
        wait_loads(right)
        for i, s, j in right:
            ub[2 * rows - 1 - i] = out[s * rows + i].astype(BF16)
        if not h:
            for i, s, j in outer:
                ub[i] = out[s * rows + i].astype(BF16)
            for v in range(SWEEPS):
                for b in range(rows + 1):
                    u_near(v, b).start()
        for i, s, j in right + ([] if h else outer):
            out[s * rows + i] = a[s * rows + i].astype(F32) * kept(i, j)
        wait_loads(below)
        for i, s, j in below:
            lb[0, rows + i] = out[s * rows + i].astype(BF16)
        if h:
            for i, s, j in outer:
                lb[0, i] = out[s * rows + i].astype(BF16)
        inverse_copy.wait()

        def lower_blocks(v):
            for i in range(1, rows):
                lower_step(i, LEFT, base + i - 1, rows + i, v, sd[v, i - 1])
            if h:
                for i in range(rows):
                    receive(D_NEAR, v, i, rd, r - 1, c)
                    lower_step(i, OUTER, i, i, v, rd[v, i])
                lower_step(0, LEFT, rows - 1, rows, v, rd[v, rows - 1])

        def diag_blocks(v):
            acc[0] = jnp.zeros((bs, bs), F32)
            for i in range(1, rows):
                u = a[RIGHT * rows + i - 1] if v else ub[2 * rows - i]
                acc[i] = dot(lb[v, rows + i], u)

            def near_terms():
                left = lb if h else rln
                for b in list(range(rows)) + [rows]:
                    receive(U_NEAR, v, b, run, r - 1, c)
                    if not h:
                        receive(L_NEAR, v, b, rln, r, c - 1)
                    i = b % rows
                    acc[i] = acc[i] + dot(left[v, b], run[v, b])

            when_near_in(near_terms)

            def finish(i, product):
                k = DIAG * rows + i
                new = a[k].astype(F32) - product
                if v + 1 < SWEEPS:
                    sd[v + 1, i] = new.astype(BF16)
                else:
                    out[k] = new * kept(i, base + i)

            @pl.when(has_far)
            def _():
                for i in range(rows):
                    receive(U_FAR, v, i, ruf, r - far_r, c)
                    receive(L_FAR, v, i, rlf, r, c - far_c)
                    finish(i, acc[i] + dot(rlf[v, i], ruf[v, i]))

            @pl.when(sends_far)
            def _():
                for i in range(rows):
                    finish(i, acc[i])
                if v + 1 < SWEEPS:
                    for i in range(rows):
                        d_far(v + 1, i).start()

            if v + 1 < SWEEPS:

                def send_near():
                    for i in range(rows):
                        d_near(v + 1, i).start()

                when_near_out(send_near)

        diag_blocks(0)
        for v in range(SWEEPS):
            lower_blocks(v)
        diag_blocks(1)

        def near_sent():
            for v in range(SWEEPS):
                for b in range(rows):
                    d_near(v, b).wait_send()

        when_near_out(near_sent)

        @pl.when(sends_far)
        def _():
            for v in range(SWEEPS):
                for b in range(rows):
                    d_far(v, b).wait_send()

        if not h:
            for v in range(SWEEPS):
                for b in range(rows + 1):
                    u_near(v, b).wait_send()

    def lower_owner(blocks, source_r, l_message, far):
        places = [(i, s, j) for i, s, j, b, n in blocks]
        start_loads(places)
        inverse_copy.start()
        hello(source_r, c)
        wait_loads(places)
        masks = {}
        for i, s, j, b, n in blocks:
            k = s * rows + i
            masks[k] = pattern[i, j].astype(F32) if far else None
            if far:
                out[k] = out[k] * masks[k]
            lb[0, b] = out[k].astype(BF16)
        pl.semaphore_wait(barrier, 1)
        for i, s, j, b, n in blocks:
            l_message(0, b).start()
        inverse_copy.wait()
        for v in range(SWEEPS):
            for i, s, j, b, n in blocks:
                if b == n:
                    receive(D_NEAR, v, n, rd, source_r, c)
                lower_step(i, s, j, b, v, rd[v, n], masks[s * rows + i])
                if v + 1 < SWEEPS:
                    l_message(v + 1, b).start()
        for v in range(SWEEPS):
            for i, s, j, b, n in blocks:
                l_message(v, b).wait_send()

    def upper_owner(blocks, u_message, far):
        places = [(i, s, j) for i, s, j, b in blocks]
        start_loads(places)
        wait_loads(places)
        for i, s, j, b in blocks:
            k = s * rows + i
            if far:
                mask = pattern[i, j].astype(F32)
                ub[b] = (out[k] * mask).astype(BF16)
                masked = a[k].astype(F32) * mask
                ua[b] = masked.astype(BF16)
                out[k] = masked * kept(i, j)
            else:
                ub[b] = out[k].astype(BF16)
                out[k] = a[k].astype(F32) * kept(i, j)
        pl.semaphore_wait(barrier, 1)
        for v in range(SWEEPS):
            for i, s, j, b in blocks:
                u_message(v, b).start()
        for v in range(SWEEPS):
            for i, s, j, b in blocks:
                u_message(v, b).wait_send()

    pl.when(q == 0)(lambda: diagonal_owner(0))
    pl.when(q == 1)(lambda: diagonal_owner(1))

    @pl.when(q == 2)
    def _():
        blocks = [(i, OUTER, rows + i, i, i) for i in range(rows)]
        lower_owner(blocks + [(0, LEFT, cols - 1, rows, rows - 1)], r - 1, l_near, False)

    @pl.when(q == -1)
    def _():
        blocks = [(i, OUTER, i, i) for i in range(rows)]
        upper_owner(blocks + [(rows - 1, RIGHT, 0, rows)], u_near, False)

    @pl.when((q == far_r) | (q == far_r + 1))
    def _():
        base = (q - far_r) * rows
        blocks = [(i, OUTER, base + i, i, i) for i in range(rows)]
        lower_owner(blocks, r - far_r, l_far, True)

    @pl.when((q == -far_r) | (q == 1 - far_r))
    def _():
        base = (q + far_r) * rows
        blocks = [(i, OUTER, base + i, i) for i in range(rows)]
        upper_owner(blocks, u_far, True)


def place_kernel(rows, cols, row_devices, bs, blocks, out, sem):
    r, c = lax.axis_index("row"), lax.axis_index("col")
    q = r - (cols // rows) * c
    far = (row_devices // 2) * rows
    copies = []
    for i in range(rows):
        for j in range(cols):
            d = rows * q + i - j
            k = jnp.where(
                d == 0, DIAG * rows + i,
                jnp.where(
                    d == 1, LEFT * rows + i,
                    jnp.where(
                        d == -1, RIGHT * rows + i,
                        jnp.where(
                            (d == rows) | (d == -rows) | (d == far) | (d == -far),
                            OUTER * rows + i, rows * SLOTS,
                        ),
                    ),
                ),
            )
            dst = out.at[pl.ds(i * bs, bs), pl.ds(j * bs, bs)]
            copies.append(pltpu.make_async_copy(blocks.at[k], dst, sem.at[i * cols + j]))
    for copy in copies:
        copy.start()
    for copy in copies:
        copy.wait()


def solution(mesh):
    row_devices, col_devices = mesh.shape["row"], mesh.shape["col"]

    def on_device(matrix, factors, inverse, pattern, dropped):
        rows, cols = pattern.shape
        bs = inverse.shape[1]
        places = rows * SLOTS
        half = lambda *n: pltpu.VMEM(n + (bs, bs), BF16)
        hbm = pl.BlockSpec(memory_space=pltpu.HBM)
        smem = pl.BlockSpec(memory_space=pltpu.SMEM)
        vmem = pl.BlockSpec(memory_space=pltpu.VMEM)
        blocks = pl.pallas_call(
            functools.partial(sweep_kernel, rows, cols, row_devices, col_devices, bs),
            out_shape=jax.ShapeDtypeStruct((places + 1, bs, bs), F32),
            in_specs=[smem, smem, hbm, hbm, hbm],
            out_specs=vmem,
            scratch_shapes=[
                half(places), half(cols), half(SWEEPS, 2 * rows), half(2 * rows), half(rows),
                half(SWEEPS, rows), half(SWEEPS, rows),
                half(SWEEPS, rows + 1), half(SWEEPS, rows + 1), half(SWEEPS, rows), half(SWEEPS, rows),
                pltpu.VMEM((rows, bs, bs), F32),
                pltpu.SemaphoreType.DMA((2, places)),
                pltpu.SemaphoreType.DMA,
                pltpu.SemaphoreType.DMA((6, SWEEPS, rows + 1)),
                pltpu.SemaphoreType.DMA((6, SWEEPS, rows + 1)),
            ],
            compiler_params=pltpu.CompilerParams(collective_id=0, has_side_effects=True),
            name="sweeps",
        )(pattern, dropped, matrix, factors, inverse)
        return pl.pallas_call(
            functools.partial(place_kernel, rows, cols, row_devices, bs),
            out_shape=jax.ShapeDtypeStruct(factors.shape, F32),
            in_specs=[vmem],
            out_specs=hbm,
            scratch_shapes=[pltpu.SemaphoreType.DMA((rows * cols,))],
            name="place",
        )(blocks)

    placed = (P("row", "col"), P("row", "col"), P("col", None, None), P("row", "col"), P("row", "col"))
    return jax.shard_map(
        on_device, mesh=mesh, in_specs=placed, out_specs=P("row", "col"), check_vma=False
    )
```

time: 18.6 us -> 21 us (1.13)
  the two profiles are of different devices: /device:TPU:20 before, /device:TPU:21 now
where the time goes in v2:
time: 21 us; the launch traced here: 20.8 us
  Pallas kernels  20.8 us (99%)
    pallas_call x1, Pallas kernels, on_device(): pl.pallas_call(functools.partial(sweep_kernel, rows, cols, row_devices, c...  18 us
    pallas_call x1, Pallas kernels, on_device(): pl.pallas_call(functools.partial(place_kernel, rows, cols, row_devices, b...  2.81 us

profile of v2, /device:TPU:21, one launch (start us, length us, event | category | flops | bytes accessed | tf_op | source)
XLA Modules:
  0.0 20.8 jit_solution(6262197751971912687)
XLA Ops:
  0.0 18.0 %sweeps.1.blocks = f32[17,128,128]{2,1,0:T(8,128)} custom-call(s32[4,8]{1,0:T(4,128)} %pattern.1, s32[4,8]{1,0:T(4,128)} %dropped.1, bf16[512,1024]{1,0:T(8,128)(2,1)} %matrix.1, f32[512,1024]{1,0:T(8,128)} %factors.1, bf16[8,128,128]{2,1,0:T(8,128)(2,1)} %inverse_in.1), custom_call_target="tpu_custom_call" | custom-call | tf_op jit(solution)/shard_map/sweeps/pallas_call | solution.py:384
  18.0 2.8 %place.1 = f32[512,1024]{1,0:T(8,128)} custom-call(f32[17,128,128]{2,1,0:T(8,128)} %sweeps.1.blocks), custom_call_target="tpu_custom_call" | custom-call | tf_op jit(solution)/shard_map/place/pallas_call | solution.py:402

commit v3 on v2

--- a/solution.py
+++ b/solution.py
@@ -55,36 +55,35 @@
     def hello(r2, c2):
         pl.semaphore_signal(barrier, inc=1, device_id=(r2, c2), device_id_type=MESH)
 
-    def message(kind, v, b, src, dst, slot, r2, c2):
+    def message(kind, v, src, dst, slot, r2, c2):
         return pltpu.make_async_remote_copy(
-            src_ref=src, dst_ref=dst.at[v, b],
-            send_sem=send_sem.at[kind, v, b], recv_sem=recv_sem.at[slot, v, b],
+            src_ref=src, dst_ref=dst.at[v],
+            send_sem=send_sem.at[kind, v], recv_sem=recv_sem.at[slot, v],
             device_id=(r2, c2), device_id_type=MESH,
         )
 
-    def receive(slot, v, b, dst, r2, c2):
-        message(slot, v, b, dst.at[v, b], dst, slot, r2, c2).wait_recv()
-
-    def d_near(v, b):
-        return message(D_NEAR, v, b, sd.at[v, b], rd, D_NEAR, r + 1, c)
-
-    def d_far(v, b):
-        return message(D_FAR, v, b, sd.at[v, b], rd, D_NEAR, r + far_r, c)
-
-    def l_near(v, b):
-        return message(L_NEAR, v, b, lb.at[v, b], rln, L_NEAR, r, c + 1)
-
-    def l_far(v, b):
-        return message(L_FAR, v, b, lb.at[v, b], rlf, L_FAR, r, c + far_c)
-
-    def u_near(v, b):
-        k = OUTER * rows + b if b < rows else RIGHT * rows + rows - 1
-        src = a.at[k] if v else ub.at[b]
-        return message(U_NEAR, v, b, src, run, U_NEAR, r + 1, c)
-
-    def u_far(v, b):
-        src = ua.at[b] if v else ub.at[b]
-        return message(U_FAR, v, b, src, ruf, U_FAR, r + far_r, c)
+    def receive(slot, v, dst, r2, c2):
+        message(slot, v, dst.at[v], dst, slot, r2, c2).wait_recv()
+
+    def d_near(v):
+        return message(D_NEAR, v, sd.at[v], rd, D_NEAR, r + 1, c)
+
+    def d_far(v):
+        return message(D_FAR, v, sd.at[v], rd, D_NEAR, r + far_r, c)
+
+    def l_near(v):
+        return message(L_NEAR, v, lb.at[v, pl.ds(0, rows + 1)], rln, L_NEAR, r, c + 1)
+
+    def l_far(v):
+        return message(L_FAR, v, lb.at[v, pl.ds(0, rows)], rlf, L_FAR, r, c + far_c)
+
+    def u_near(v):
+        src = a.at[pl.ds(OUTER * rows - 1, rows + 1)] if v else ub.at[pl.ds(0, rows + 1)]
+        return message(U_NEAR, v, src, run, U_NEAR, r + 1, c)
+
+    def u_far(v):
+        src = ua if v else ub.at[pl.ds(1, rows)]
+        return message(U_FAR, v, src, ruf, U_FAR, r + far_r, c)
 
     def kept(i, j):
         return (1 - dropped[i, j]).astype(F32)
@@ -104,8 +103,6 @@
         else:
             out[k] = new * kept(i, j)
 
-    out[rows * SLOTS] = jnp.zeros((bs, bs), F32)
-
     def diagonal_owner(h):
         base = h * rows
         below = [(i, LEFT, base + i - 1) for i in range(rows) if base + i >= 1]
@@ -156,24 +153,21 @@
 
         @pl.when(sends_far)
         def _():
-            for b in range(rows):
-                d_far(0, b).start()
+            d_far(0).start()
 
         def send_first_near():
-            for b in range(rows):
-                d_near(0, b).start()
+            d_near(0).start()
 
         when_near_out(send_first_near)
         wait_loads(outer)
         wait_loads(right)
         for i, s, j in right:
-            ub[2 * rows - 1 - i] = out[s * rows + i].astype(BF16)
+            ub[0 if i == rows - 1 else rows + 1 + i] = out[s * rows + i].astype(BF16)
         if not h:
             for i, s, j in outer:
-                ub[i] = out[s * rows + i].astype(BF16)
+                ub[1 + i] = out[s * rows + i].astype(BF16)
             for v in range(SWEEPS):
-                for b in range(rows + 1):
-                    u_near(v, b).start()
+                u_near(v).start()
         for i, s, j in right + ([] if h else outer):
             out[s * rows + i] = a[s * rows + i].astype(F32) * kept(i, j)
         wait_loads(below)
@@ -188,25 +182,25 @@
             for i in range(1, rows):
                 lower_step(i, LEFT, base + i - 1, rows + i, v, sd[v, i - 1])
             if h:
+                receive(D_NEAR, v, rd, r - 1, c)
                 for i in range(rows):
-                    receive(D_NEAR, v, i, rd, r - 1, c)
                     lower_step(i, OUTER, i, i, v, rd[v, i])
                 lower_step(0, LEFT, rows - 1, rows, v, rd[v, rows - 1])
 
         def diag_blocks(v):
             acc[0] = jnp.zeros((bs, bs), F32)
             for i in range(1, rows):
-                u = a[RIGHT * rows + i - 1] if v else ub[2 * rows - i]
+                u = a[RIGHT * rows + i - 1] if v else ub[rows + i]
                 acc[i] = dot(lb[v, rows + i], u)
 
             def near_terms():
                 left = lb if h else rln
-                for b in list(range(rows)) + [rows]:
-                    receive(U_NEAR, v, b, run, r - 1, c)
-                    if not h:
-                        receive(L_NEAR, v, b, rln, r, c - 1)
-                    i = b % rows
-                    acc[i] = acc[i] + dot(left[v, b], run[v, b])
+                receive(U_NEAR, v, run, r - 1, c)
+                if not h:
+                    receive(L_NEAR, v, rln, r, c - 1)
+                acc[0] = acc[0] + dot(left[v, rows], run[v, 0])
+                for i in range(rows):
+                    acc[i] = acc[i] + dot(left[v, i], run[v, 1 + i])
 
             when_near_in(near_terms)
 
@@ -220,9 +214,9 @@
 
             @pl.when(has_far)
             def _():
+                receive(U_FAR, v, ruf, r - far_r, c)
+                receive(L_FAR, v, rlf, r, c - far_c)
                 for i in range(rows):
-                    receive(U_FAR, v, i, ruf, r - far_r, c)
-                    receive(L_FAR, v, i, rlf, r, c - far_c)
                     finish(i, acc[i] + dot(rlf[v, i], ruf[v, i]))
 
             @pl.when(sends_far)
@@ -230,16 +224,10 @@
                 for i in range(rows):
                     finish(i, acc[i])
                 if v + 1 < SWEEPS:
-                    for i in range(rows):
-                        d_far(v + 1, i).start()
+                    d_far(v + 1).start()
 
             if v + 1 < SWEEPS:
-
-                def send_near():
-                    for i in range(rows):
-                        d_near(v + 1, i).start()
-
-                when_near_out(send_near)
+                when_near_out(lambda: d_near(v + 1).start())
 
         diag_blocks(0)
         for v in range(SWEEPS):
@@ -248,21 +236,18 @@
 
         def near_sent():
             for v in range(SWEEPS):
-                for b in range(rows):
-                    d_near(v, b).wait_send()
+                d_near(v).wait_send()
 
         when_near_out(near_sent)
 
         @pl.when(sends_far)
         def _():
             for v in range(SWEEPS):
-                for b in range(rows):
-                    d_far(v, b).wait_send()
+                d_far(v).wait_send()
 
         if not h:
             for v in range(SWEEPS):
-                for b in range(rows + 1):
-                    u_near(v, b).wait_send()
+                u_near(v).wait_send()
 
     def lower_owner(blocks, source_r, l_message, far):
         places = [(i, s, j) for i, s, j, b, n in blocks]
@@ -278,19 +263,16 @@
                 out[k] = out[k] * masks[k]
             lb[0, b] = out[k].astype(BF16)
         pl.semaphore_wait(barrier, 1)
-        for i, s, j, b, n in blocks:
-            l_message(0, b).start()
+        l_message(0).start()
         inverse_copy.wait()
         for v in range(SWEEPS):
+            receive(D_NEAR, v, rd, source_r, c)
             for i, s, j, b, n in blocks:
-                if b == n:
-                    receive(D_NEAR, v, n, rd, source_r, c)
                 lower_step(i, s, j, b, v, rd[v, n], masks[s * rows + i])
-                if v + 1 < SWEEPS:
-                    l_message(v + 1, b).start()
-        for v in range(SWEEPS):
-            for i, s, j, b, n in blocks:
-                l_message(v, b).wait_send()
+            if v + 1 < SWEEPS:
+                l_message(v + 1).start()
+        for v in range(SWEEPS):
+            l_message(v).wait_send()
 
     def upper_owner(blocks, u_message, far):
         places = [(i, s, j) for i, s, j, b in blocks]
@@ -302,18 +284,16 @@
                 mask = pattern[i, j].astype(F32)
                 ub[b] = (out[k] * mask).astype(BF16)
                 masked = a[k].astype(F32) * mask
-                ua[b] = masked.astype(BF16)
+                ua[b - 1] = masked.astype(BF16)
                 out[k] = masked * kept(i, j)
             else:
                 ub[b] = out[k].astype(BF16)
                 out[k] = a[k].astype(F32) * kept(i, j)
         pl.semaphore_wait(barrier, 1)
         for v in range(SWEEPS):
-            for i, s, j, b in blocks:
-                u_message(v, b).start()
-        for v in range(SWEEPS):
-            for i, s, j, b in blocks:
-                u_message(v, b).wait_send()
+            u_message(v).start()
+        for v in range(SWEEPS):
+            u_message(v).wait_send()
 
     pl.when(q == 0)(lambda: diagonal_owner(0))
     pl.when(q == 1)(lambda: diagonal_owner(1))
@@ -325,8 +305,8 @@
 
     @pl.when(q == -1)
     def _():
-        blocks = [(i, OUTER, i, i) for i in range(rows)]
-        upper_owner(blocks + [(rows - 1, RIGHT, 0, rows)], u_near, False)
+        blocks = [(i, OUTER, i, 1 + i) for i in range(rows)]
+        upper_owner(blocks + [(rows - 1, RIGHT, 0, 0)], u_near, False)
 
     @pl.when((q == far_r) | (q == far_r + 1))
     def _():
@@ -337,37 +317,35 @@
     @pl.when((q == -far_r) | (q == 1 - far_r))
     def _():
         base = (q + far_r) * rows
-        blocks = [(i, OUTER, base + i, i) for i in range(rows)]
+        blocks = [(i, OUTER, base + i, 1 + i) for i in range(rows)]
         upper_owner(blocks, u_far, True)
 
 
-def place_kernel(rows, cols, row_devices, bs, blocks, out, sem):
+def place_kernel(rows, cols, row_devices, bs, blocks, out, held, zero, load_sem, sem):
     r, c = lax.axis_index("row"), lax.axis_index("col")
     q = r - (cols // rows) * c
     far = (row_devices // 2) * rows
-    copies = []
+    load = pltpu.make_async_copy(blocks, held, load_sem)
+    load.start()
+    zero[...] = jnp.zeros_like(zero)
+    places = []
     for i in range(rows):
         for j in range(cols):
             d = rows * q + i - j
-            k = jnp.where(
-                d == 0, DIAG * rows + i,
-                jnp.where(
-                    d == 1, LEFT * rows + i,
-                    jnp.where(
-                        d == -1, RIGHT * rows + i,
-                        jnp.where(
-                            (d == rows) | (d == -rows) | (d == far) | (d == -far),
-                            OUTER * rows + i, rows * SLOTS,
-                        ),
-                    ),
-                ),
+            outer = (d == rows) | (d == -rows) | (d == far) | (d == -far)
+            near = (d == 0) | (d == 1) | (d == -1)
+            slot = jnp.where(
+                d == 0, DIAG, jnp.where(d == 1, LEFT, jnp.where(d == -1, RIGHT, OUTER))
             )
             dst = out.at[pl.ds(i * bs, bs), pl.ds(j * bs, bs)]
-            copies.append(pltpu.make_async_copy(blocks.at[k], dst, sem.at[i * cols + j]))
-    for copy in copies:
-        copy.start()
-    for copy in copies:
-        copy.wait()
+            places.append((outer | near, slot * rows + i, dst, sem.at[i * cols + j]))
+    for kept, k, dst, done in places:
+        pl.when(~kept)(lambda: pltpu.make_async_copy(zero, dst, done).start())
+    load.wait()
+    for kept, k, dst, done in places:
+        pl.when(kept)(lambda: pltpu.make_async_copy(held.at[k], dst, done).start())
+    for kept, k, dst, done in places:
+        pltpu.make_async_copy(zero, dst, done).wait()
 
 
 def solution(mesh):
@@ -383,7 +361,7 @@
         vmem = pl.BlockSpec(memory_space=pltpu.VMEM)
         blocks = pl.pallas_call(
             functools.partial(sweep_kernel, rows, cols, row_devices, col_devices, bs),
-            out_shape=jax.ShapeDtypeStruct((places + 1, bs, bs), F32),
+            out_shape=jax.ShapeDtypeStruct((places, bs, bs), F32),
             in_specs=[smem, smem, hbm, hbm, hbm],
             out_specs=vmem,
             scratch_shapes=[
@@ -393,8 +371,8 @@
                 pltpu.VMEM((rows, bs, bs), F32),
                 pltpu.SemaphoreType.DMA((2, places)),
                 pltpu.SemaphoreType.DMA,
-                pltpu.SemaphoreType.DMA((6, SWEEPS, rows + 1)),
-                pltpu.SemaphoreType.DMA((6, SWEEPS, rows + 1)),
+                pltpu.SemaphoreType.DMA((6, SWEEPS)),
+                pltpu.SemaphoreType.DMA((6, SWEEPS)),
             ],
             compiler_params=pltpu.CompilerParams(collective_id=0, has_side_effects=True),
             name="sweeps",
@@ -402,9 +380,14 @@
         return pl.pallas_call(
             functools.partial(place_kernel, rows, cols, row_devices, bs),
             out_shape=jax.ShapeDtypeStruct(factors.shape, F32),
-            in_specs=[vmem],
+            in_specs=[hbm],
             out_specs=hbm,
-            scratch_shapes=[pltpu.SemaphoreType.DMA((rows * cols,))],
+            scratch_shapes=[
+                pltpu.VMEM((places, bs, bs), F32),
+                pltpu.VMEM((bs, bs), F32),
+                pltpu.SemaphoreType.DMA,
+                pltpu.SemaphoreType.DMA((rows * cols,)),
+            ],
             name="place",
         )(blocks)
 

time: 21 us -> 18.6 us (0.89)
  the two profiles are of different devices: /device:TPU:21 before, /device:TPU:20 now
where the time goes in v3:
time: 18.6 us; the launch traced here: 18.4 us
  Pallas kernels  18.4 us (99%)
    pallas_call x1, Pallas kernels, on_device(): pl.pallas_call(functools.partial(sweep_kernel, rows, cols, row_devices, c...  15.5 us
    pallas_call x1, Pallas kernels, on_device(): pl.pallas_call(functools.partial(place_kernel, rows, cols, row_devices, b...  2.88 us

profile of v3, /device:TPU:20, one launch (start us, length us, event | category | flops | bytes accessed | tf_op | source)
XLA Modules:
  0.0 18.4 jit_solution(1559176923576972510)
XLA Ops:
  0.0 15.5 %sweeps.1.blocks = f32[16,128,128]{2,1,0:T(8,128)} custom-call(s32[4,8]{1,0:T(4,128)} %pattern.1, s32[4,8]{1,0:T(4,128)} %dropped.1, bf16[512,1024]{1,0:T(8,128)(2,1)} %matrix.1, f32[512,1024]{1,0:T(8,128)} %factors.1, bf16[8,128,128]{2,1,0:T(8,128)(2,1)} %inverse_in.1), custom_call_target="tpu_custom_call" | custom-call | tf_op jit(solution)/shard_map/sweeps/pallas_call | solution.py:362
  15.5 2.9 %place.1 = f32[512,1024]{1,0:T(8,128)} custom-call(f32[16,128,128]{2,1,0:T(8,128)} %sweeps.1.blocks), custom_call_target="tpu_custom_call" | custom-call | tf_op jit(solution)/shard_map/place/pallas_call | solution.py:380
